TPU v7x, 32 devices: a whole 2x2x4 slice. The times are simulated.
32 devices in a mesh: space: 8 (over z, y), tm: 4 (over x, core).
Axes of the slice: x: 2, y: 2, z: 4, core: 2. Of those that a mesh axis runs over, the one named last changes fastest.
Arguments:
- precip: float32 [512, 48, 2048], P('tm', 'space'), may hold values from 0.0001 to 0.01
Outputs:
- totals: float32 [48, 2048, 512], P(None, 'space', 'tm')
All inputs are finite; a program needn't handle non-finite values.
Results may differ from a plain program's by a relative error of at most 0.00005.
Values sent between devices are 32-bit elements; how exact they have to be, the bound alone decides.
A program may use at most 64 MiB of HBM per device.

v0:
```python
import jax
import jax.numpy as jnp
from jax import lax
from jax.sharding import PartitionSpec as P


def entering(part, axis, combine, identity):
    place = lax.axis_index(axis)
    gathered = lax.all_gather(part, axis)
    state = jnp.zeros_like(part) + jnp.asarray(identity, part.dtype)

    def one(turn, state):
        return combine(state, lax.dynamic_index_in_dim(gathered, turn, 0, False))

    return lax.fori_loop(0, place, one, state)


def rechunk(source):
    return lax.all_to_all(source, "space", split_axis=2, concat_axis=1, tiled=True)


def add_terms(earlier_part, later_part):
    return earlier_part + later_part


def day_prefix(pixel_major, upper_ones):
    lat_rows, lon_cols, day_count = pixel_major.shape
    flat_rows = pixel_major.reshape(lat_rows * lon_cols, day_count)
    summed = jnp.dot(
        flat_rows, upper_ones, precision=lax.Precision.HIGHEST, preferred_element_type=jnp.float32
    )
    return summed.reshape(lat_rows, lon_cols, day_count)


def per_device(precip):
    day_count = precip.shape[0]
    position = lax.broadcasted_iota(jnp.int32, (day_count, day_count), 0)
    later_pos = lax.broadcasted_iota(jnp.int32, (day_count, day_count), 1)
    upper_ones = (position <= later_pos).astype(jnp.float32)
    pixel_major = jnp.transpose(rechunk(precip), (1, 2, 0))
    running = day_prefix(pixel_major, upper_ones)
    last_day = running[:, :, -1]
    carried = entering(last_day, "tm", add_terms, jnp.zeros_like(last_day))
    return running + carried[:, :, None]


def solution(mesh):
    return jax.shard_map(
        per_device,
        mesh=mesh,
        in_specs=(P("tm", "space", None),),
        out_specs=P(None, "space", "tm"),
        check_vma=False,
    )
```

profile of v0, /device:TPU:0, one launch (start us, length us, event | category | flops | bytes accessed | tf_op | source)
XLA Modules:
  0.0 231.7 jit_solution(16729160938471448487)
XLA Ops:
  0.0 8.4 %copy.8 = f32[128,6,2048]{0,1,2:T(8,128)} copy(f32[128,6,2048]{2,0,1:T(8,128)} %param.3) | data formatting | bytes 12582912 | tf_op args[0]
  8.4 7.3 %all-to-all-start = ((f32[128,6,2048]{0,1,2:T(8,128)}), f32[128,6,2048]{0,1,2:T(8,128)}, u32[]{:S(2)}, u32[]{:S(2)}) async-start(f32[128,6,2048]{0,1,2:T(8,128)} %copy.8), calls=%async_computation | async-start | bytes 16777216 | tf_op jit(solution)/shard_map/all_to_all | solution.py:19
  15.7 183.2 %all-to-all-done = f32[128,6,2048]{0,1,2:T(8,128)} async-done(((f32[128,6,2048]{0,1,2:T(8,128)}), f32[128,6,2048]{0,1,2:T(8,128)}, u32[]{:S(2)}, u32[]{:S(2)}) %all-to-all-start) | async-done | bytes 6291488 | tf_op jit(solution)/shard_map/all_to_all | solution.py:19
  198.9 4.5 %copy.14 = f32[128,8,6,256]{0,3,2,1:T(8,128)S(1)} copy(f32[128,8,6,256]{0,2,3,1:T(8,128)} %bitcast.3) | data formatting | bytes 12582912 | tf_op jit(solution)/shard_map/transpose | solution.py:40
  203.4 3.3 %fusion.1 = f32[128,12288]{1,0:T(8,128)S(1)} fusion(f32[12288,128]{1,0:T(8,128)S(1)} %bitcast.21), kind=kOutput, calls=%fused_computation.4 | convolution fusion | flops 2415951872 | bytes 12582912 | tf_op jit(solution)/shard_map/dot_general | solution.py:29
  206.7 4.7 %copy.15 = f32[16,8,48,256]{3,2,1,0:T(8,128)} copy(f32[16,8,48,256]{3,1,2,0:T(8,128)S(1)} %bitcast.22) | data formatting | bytes 12582912
  211.3 6.7 %copy.12 = f32[48,256,128]{2,1,0:T(8,128)} copy(f32[48,256,128]{1,0,2:T(8,128)} %bitcast.19) | data formatting | bytes 12582912 | tf_op jit(solution)/shard_map/reshape | solution.py:32
  218.0 0.8 slice.4
  218.8 5.6 %all-gather = f32[192,256,1]{1,0,2:T(8,128)S(1)} all-gather(f32[48,256,1]{1,0,2:T(8,128)S(1)} %slice.4), channel_id=2, replica_groups=mesh['space'=8,'tm'=4] {'tm'}, dimensions={0}, use_global_device_ids=true | all-gather | bytes 245760 | tf_op jit(solution)/shard_map/all_gather | solution.py:9
  224.4 7.2 %broadcast_add_fusion = f32[48,256,128]{2,1,0:T(8,128)} fusion(f32[48,256,128]{2,1,0:T(8,128)} %copy.12, f32[48,256]{1,0:T(8,128)S(1)} %get-tuple-element.28), kind=kLoop, calls=%fused_computation.1 | loop fusion | flops 1572864 | bytes 12632064 | tf_op jit(solution)/shard_map/add | solution.py:44
  (2 shorter events, 0.0 us)
Async XLA Ops:
  8.4 190.5 %all-to-all-start = ((f32[128,6,2048]{0,1,2:T(8,128)}), f32[128,6,2048]{0,1,2:T(8,128)}, u32[]{:S(2)}, u32[]{:S(2)}) async-start(f32[128,6,2048]{0,1,2:T(8,128)} %copy.8), calls=%async_computation | async-start | bytes 16777216 | tf_op jit(solution)/shard_map/all_to_all | solution.py:19
where the time goes:
time: 232 us
  waiting for transfers between devices  183 us (79%)
  local copies, waits for them, and re-layouts  25 us (11%)
  starting transfers between devices  7.31 us (3%)
  other arithmetic  7.24 us (3%)
  blocking collectives  5.58 us (2%)
  matrix products  3.3 us (1%)
    all_to_all x1, waiting for transfers between devices, rechunk(): lax.all_to_all(source, 'space', split_axis=2, concat_axis=1, tiled=True)  183 us
    unnamed x2, local copies, waits for them, and re-layouts  13.1 us
    all_to_all x1, starting transfers between devices, rechunk(): lax.all_to_all(source, 'space', split_axis=2, concat_axis=1, tiled=True)  7.31 us
    add x1, other arithmetic, per_device(): return running + carried[:, :, None]  7.24 us
    reshape x1, local copies, waits for them, and re-layouts, day_prefix(): return summed.reshape(lat_rows, lon_cols, day_count)  6.69 us
    all_gather x1, blocking collectives, entering(): gathered = lax.all_gather(part, axis)  5.58 us
  transfers between devices with their start and end apart: 1, of which 1 were waited for; matrix products, arithmetic and copies ran while one was open for 0% of the time, Pallas kernels for 0%

commit v1 on v0

--- a/solution.py
+++ b/solution.py
@@ -16,7 +16,10 @@
 
 
 def rechunk(source):
-    return lax.all_to_all(source, "space", split_axis=2, concat_axis=1, tiled=True)
+    return jnp.concatenate(
+        lax.all_to_all(jnp.stack(jnp.split(source, lax.axis_size("space"), axis=2)), "space", 0, 0),
+        axis=1,
+    )
 
 
 def add_terms(earlier_part, later_part):

time: 232 us -> 197 us (0.85)
  waiting for transfers between devices: 183 us -> 138 us
  local copies, waits for them, and re-layouts: 25 us -> 32.6 us
  matrix products: 3.3 us -> 6.29 us
    all_to_all x1, waiting for transfers between devices: 183 us -> 138 us  [rechunk(): lax.all_to_all(jnp.stack(jnp.split(source, lax.axis_size('space'), axis=2...]
    add x0 -> x1, local copies, waits for them, and re-layouts: none -> 6.55 us  [per_device(): return running + carried[:, :, None]]
    transpose x1 -> x0, local copies, waits for them, and re-layouts: 4.5 us -> none  [per_device(): pixel_major = jnp.transpose(rechunk(precip), (1, 2, 0))]
    unnamed x2 -> x10, local copies, waits for them, and re-layouts: 13.1 us -> 17.4 us
    dot_general x1, matrix products: 3.3 us -> 6.29 us  [day_prefix(): jnp.dot(flat_rows, upper_ones, precision=lax.Precision.HIGHEST, preferred...]
where the time goes in v1:
time: 197 us
  waiting for transfers between devices  138 us (70%)
  local copies, waits for them, and re-layouts  32.6 us (17%)
  starting transfers between devices  7.31 us (4%)
  other arithmetic  6.66 us (3%)
  matrix products  6.29 us (3%)
  blocking collectives  5.6 us (3%)
    all_to_all x1, waiting for transfers between devices, rechunk(): lax.all_to_all(jnp.stack(jnp.split(source, lax.axis_size('space'), axis=2...  138 us
    unnamed x10, local copies, waits for them, and re-layouts  17.4 us
    all_to_all x1, starting transfers between devices, rechunk(): lax.all_to_all(jnp.stack(jnp.split(source, lax.axis_size('space'), axis=2...  7.31 us
    add x1, other arithmetic, per_device(): return running + carried[:, :, None]  6.66 us
    reshape x1, local copies, waits for them, and re-layouts, rechunk(): jnp.concatenate(lax.all_to_all(jnp.stack(jnp.split(source, lax.axis_size(...  6.55 us
    add x1, local copies, waits for them, and re-layouts, per_device(): return running + carried[:, :, None]  6.55 us
    dot_general x1, matrix products, day_prefix(): jnp.dot(flat_rows, upper_ones, precision=lax.Precision.HIGHEST, preferred...  6.29 us
    all_gather x1, blocking collectives, entering(): gathered = lax.all_gather(part, axis)  5.6 us
  transfers between devices with their start and end apart: 1, of which 1 were waited for; matrix products, arithmetic and copies ran while one was open for 0% of the time, Pallas kernels for 0%

profile of v1, /device:TPU:0, one launch (start us, length us, event | category | flops | bytes accessed | tf_op | source)
XLA Modules:
  0.0 196.8 jit_solution(10137044305256790408)
XLA Ops:
  0.0 2.1 %bitcast_dynamic-update-slice_fusion.7 = f32[8,128,6,256]{3,1,2,0:T(8,128)} fusion(f32[128,6,2048]{2,0,1:T(8,128)} %param.3), kind=kLoop, calls=%fused_computation.9 | loop fusion | bytes 1572864
  2.1 2.1 %bitcast_dynamic-update-slice_fusion.6 = f32[8,128,6,256]{3,1,2,0:T(8,128)} fusion(f32[8,128,6,256]{3,1,2,0:T(8,128)} %bitcast_dynamic-update-slice_fusion.7, f32[128,6,2048]{2,0,1:T(8,128)} %param.3), kind=kLoop, calls=%fused_computation.8 | loop fusion | bytes 1572864
  4.2 2.1 %bitcast_dynamic-update-slice_fusion.5 = f32[8,128,6,256]{3,1,2,0:T(8,128)} fusion(f32[8,128,6,256]{3,1,2,0:T(8,128)} %bitcast_dynamic-update-slice_fusion.6, f32[128,6,2048]{2,0,1:T(8,128)} %param.3), kind=kLoop, calls=%fused_computation.7 | loop fusion | bytes 1572864
  6.3 2.1 %bitcast_dynamic-update-slice_fusion.4 = f32[8,128,6,256]{3,1,2,0:T(8,128)} fusion(f32[8,128,6,256]{3,1,2,0:T(8,128)} %bitcast_dynamic-update-slice_fusion.5, f32[128,6,2048]{2,0,1:T(8,128)} %param.3), kind=kLoop, calls=%fused_computation.6 | loop fusion | bytes 1572864
  8.4 2.1 %bitcast_dynamic-update-slice_fusion.3 = f32[8,128,6,256]{3,1,2,0:T(8,128)} fusion(f32[8,128,6,256]{3,1,2,0:T(8,128)} %bitcast_dynamic-update-slice_fusion.4, f32[128,6,2048]{2,0,1:T(8,128)} %param.3), kind=kLoop, calls=%fused_computation.5 | loop fusion | bytes 1572864
  10.5 2.1 %bitcast_dynamic-update-slice_fusion.2 = f32[8,128,6,256]{3,1,2,0:T(8,128)} fusion(f32[8,128,6,256]{3,1,2,0:T(8,128)} %bitcast_dynamic-update-slice_fusion.3, f32[128,6,2048]{2,0,1:T(8,128)} %param.3), kind=kLoop, calls=%fused_computation.4 | loop fusion | bytes 1572864
  12.6 2.1 %bitcast_dynamic-update-slice_fusion.1 = f32[8,128,6,256]{3,1,2,0:T(8,128)} fusion(f32[8,128,6,256]{3,1,2,0:T(8,128)} %bitcast_dynamic-update-slice_fusion.2, f32[128,6,2048]{2,0,1:T(8,128)} %param.3), kind=kLoop, calls=%fused_computation.3 | loop fusion | bytes 1572864
  14.7 2.1 %bitcast_dynamic-update-slice_fusion = f32[8,128,6,256]{3,1,2,0:T(8,128)} fusion(f32[8,128,6,256]{3,1,2,0:T(8,128)} %bitcast_dynamic-update-slice_fusion.1, f32[128,6,2048]{2,0,1:T(8,128)} %param.3), kind=kLoop, calls=%fused_computation.2 | loop fusion | bytes 1572864 | tf_op jit(solution)/shard_map/stack | solution.py:20
  16.8 7.3 %all-to-all-start = ((f32[8,128,6,256]{3,1,2,0:T(8,128)}), f32[8,128,6,256]{3,1,2,0:T(8,128)}, u32[]{:S(2)}, u32[]{:S(2)}) async-start(f32[8,128,6,256]{3,1,2,0:T(8,128)} %bitcast_dynamic-update-slice_fusion), calls=%async_computation | async-start | bytes 12582912 | tf_op jit(solution)/shard_map/all_to_all | solution.py:20
  24.1 138.2 %all-to-all-done = f32[8,128,6,256]{3,1,2,0:T(8,128)} async-done(((f32[8,128,6,256]{3,1,2,0:T(8,128)}), f32[8,128,6,256]{3,1,2,0:T(8,128)}, u32[]{:S(2)}, u32[]{:S(2)}) %all-to-all-start) | async-done | bytes 6291488 | tf_op jit(solution)/shard_map/all_to_all | solution.py:20
  162.3 6.6 %copy.4 = f32[128,8,6,256]{0,3,2,1:T(8,128)} copy(f32[128,8,6,256]{3,0,2,1:T(8,128)} %bitcast.9) | data formatting | bytes 12582912 | tf_op jit(solution)/shard_map/reshape | solution.py:19
  168.9 6.3 %fusion.1 = f32[48,256,128]{1,2,0:T(8,128)S(1)} fusion(f32[48,256,128]{2,1,0:T(8,128)} %bitcast.29), kind=kOutput, calls=%fused_computation.12 | convolution fusion | flops 2415935488 | bytes 12582912 | tf_op jit(solution)/shard_map/dot_general | solution.py:32
  175.2 0.0 copy-start
  175.2 2.7 %copy-done = f32[48,256,128]{1,2,0:T(8,128)} copy-done((f32[48,256,128]{1,2,0:T(8,128)}, f32[48,256,128]{1,2,0:T(8,128)S(1)}, u32[]{:S(2)}) %copy-start) | copy-done | bytes 6291480
  177.9 0.1 slice.4
  177.9 5.6 %all-gather = f32[192,256,1]{1,2,0:T(1,128)S(1)} all-gather(f32[48,256,1]{1,2,0:T(1,128)S(1)} %slice.4), channel_id=2, replica_groups=mesh['space'=8,'tm'=4] {'tm'}, dimensions={0}, use_global_device_ids=true | all-gather | bytes 245760 | tf_op jit(solution)/shard_map/all_gather | solution.py:9
  183.6 6.7 %broadcast_add_fusion = f32[48,256,128]{1,2,0:T(8,128)} fusion(f32[48,256,128]{1,2,0:T(8,128)} %copy-done, f32[48,256]{1,0:T(8,128)S(1)} %get-tuple-element.28), kind=kLoop, calls=%fused_computation.1 | loop fusion | flops 1572864 | bytes 12632064 | tf_op jit(solution)/shard_map/add | solution.py:47
  190.2 6.6 %copy.5 = f32[48,256,128]{2,1,0:T(8,128)} copy(f32[48,256,128]{1,2,0:T(8,128)} %broadcast_add_fusion) | data formatting | bytes 12582912 | tf_op jit(solution)/shard_map/add | solution.py:47
  (3 shorter events, 0.0 us)
Async XLA Ops:
  16.8 145.5 %all-to-all-start = ((f32[8,128,6,256]{3,1,2,0:T(8,128)}), f32[8,128,6,256]{3,1,2,0:T(8,128)}, u32[]{:S(2)}, u32[]{:S(2)}) async-start(f32[8,128,6,256]{3,1,2,0:T(8,128)} %bitcast_dynamic-update-slice_fusion), calls=%async_computation | async-start | bytes 12582912 | tf_op jit(solution)/shard_map/all_to_all | solution.py:20
  175.2 2.7 %copy-start = (f32[48,256,128]{1,2,0:T(8,128)}, f32[48,256,128]{1,2,0:T(8,128)S(1)}, u32[]{:S(2)}) copy-start(f32[48,256,128]{1,2,0:T(8,128)S(1)} %fusion.1) | copy-start | bytes 18874372
